TPU v7x, 64 devices: a 2x2x8 block of a 4x4x8 slice. The times are simulated.
64 devices in a mesh: dp: 8 (over x, y, core), tp: 8 (over z).
Axes of the slice: x: 2, y: 2, z: 8, core: 2. Of those that a mesh axis runs over, the one named last changes fastest.
The devices are a block of a 4x4x8 slice.
Arguments:
- x: bfloat16 [16384, 2048], P('dp'), parts along dimension 0
- w_gate: bfloat16 [2048, 16384], P(None, 'tp')
- w_up: bfloat16 [2048, 16384], P(None, 'tp')
- w_down: bfloat16 [16384, 2048], P('tp')
Outputs:
- output: bfloat16 [16384, 2048], P('dp'), parts along dimension 0
There are 8 independent parts. A program takes and returns all parts, laid end to end along the dimension named above; an argument that names none is the same for every part.
All inputs are finite; a program needn't handle non-finite values.
Results may differ from a plain program's by a relative error of at most 0.016.
Values are sent between devices in bfloat16 or wider.
A program may use at most 768 MiB of HBM per device.

v0:
```python
import jax
import jax.numpy as jnp
from jax import lax
from jax.sharding import PartitionSpec as P


def solution(mesh):
    def step(x, w_gate, w_up, w_down):
        gate = jnp.dot(x, w_gate, preferred_element_type=jnp.float32)
        up = jnp.dot(x, w_up, preferred_element_type=jnp.float32)
        hidden = (jax.nn.gelu(gate) * up).astype(jnp.bfloat16)
        term = jnp.dot(hidden, w_down, preferred_element_type=jnp.float32).astype(jnp.bfloat16)
        return lax.psum(term, "tp")

    return jax.shard_map(
        step,
        mesh=mesh,
        in_specs=(P("dp", None), P(None, "tp"), P(None, "tp"), P("tp", None)),
        out_specs=P("dp", None),
        check_vma=False,
    )
```

profile of v0, /device:TPU:21, one launch (start us, length us, event | category | flops | bytes accessed | tf_op | source)
XLA Modules:
  0.0 279.9 jit_solution(6642218861781987936)
XLA Ops:
  6.5 0.0 all-reduce.2.cloned.1.call-start
  6.6 0.0 copy-start
  6.6 0.0 copy-start.1
  6.6 24.3 %fusion.13 = f32[2048,2048]{1,0:T(8,128)} fusion(bf16[2048,2048]{1,0:T(8,128)(2,1)} %param.4, bf16[2048,2048]{1,0:T(8,128)(2,1)} %param.5), kind=kOutput, calls=%fused_computation.15 | convolution fusion | flops 17179869184 | bytes 33554432 | tf_op jit(solution)/shard_map/dot_general | solution.py:9
  30.8 0.0 copy-done
  30.8 0.0 copy-done.1
  30.8 24.4 %fusion.8.clone.4 = bf16[2048,2048]{1,0:T(8,128)(2,1)} fusion(f32[2048,2048]{1,0:T(8,128)} %fusion.13, bf16[2048,2048]{1,0:T(8,128)(2,1)S(1)} %copy-done, bf16[2048,2048]{1,0:T(8,128)(2,1)S(1)} %copy-done.1), kind=kOutput, calls=%fused_computation.9.clone.clone.clone.1 | convolution fusion | flops 17221812224 | bytes 41943040 | tf_op jit(solution)/shard_map/dot_general | solution.py:10
  55.2 23.6 %convolution_convert_fusion = bf16[2048,2048]{1,0:T(8,128)(2,1)} fusion(bf16[2048,2048]{1,0:T(8,128)(2,1)} %param.7, bf16[2048,2048]{1,0:T(8,128)(2,1)} %fusion.8.clone.4), kind=kOutput, calls=%fused_computation.10 | convolution fusion | flops 17184063488 | bytes 25165824 | tf_op jit(solution)/shard_map/dot_general | solution.py:12
  78.8 0.1 all-reduce.2.cloned.1.call-update
  78.8 185.8 %all-reduce.2.cloned.1.call-done = bf16[2048,2048]{1,0:T(8,128)(2,1)} async-done(((bf16[2048,2048]{1,0:T(8,128)(2,1)}), bf16[2048,2048]{1,0:T(8,128)(2,1)}) %all-reduce.2.cloned.1.call-update) | async-done | bytes 8388624 | tf_op jit(solution)/shard_map/psum | solution.py:13
  264.6 8.4 %copy.6 = bf16[2048,2048]{1,0:T(8,128)(2,1)} copy(bf16[2048,2048]{1,0:T(8,128)(2,1)} %all-reduce.2.cloned.1.call-done) | data formatting | bytes 16777216
Async XLA Ops:
  6.5 258.0 %all-reduce.2.cloned.1.call-start = ((), (), s32[]{:S(2)}) async-start(), calls=%async_computation | async-start | bytes 16777216 | tf_op jit(solution)/shard_map/psum | solution.py:13
  6.6 24.3 %copy-start = (bf16[2048,2048]{1,0:T(8,128)(2,1)S(1)}, bf16[2048,2048]{1,0:T(8,128)(2,1)}, u32[]{:S(2)}) copy-start(bf16[2048,2048]{1,0:T(8,128)(2,1)} %param.4) | copy-start | bytes 25165828
  6.6 24.3 %copy-start.1 = (bf16[2048,2048]{1,0:T(8,128)(2,1)S(1)}, bf16[2048,2048]{1,0:T(8,128)(2,1)}, u32[]{:S(2)}) copy-start(bf16[2048,2048]{1,0:T(8,128)(2,1)} %param.6) | copy-start | bytes 25165828
Sparse Core Ops, SparseCore 0:
  78.9 185.5 all-reduce.1
where the time goes:
time: 280 us
  waiting for transfers between devices  186 us (66%)
  matrix products  72.2 us (26%)
  between operations  13.4 us (5%)
  local copies, waits for them, and re-layouts  8.45 us (3%)
    psum x1, waiting for transfers between devices, step(): return lax.psum(term, 'tp')  186 us
    dot_general x1, matrix products, step(): up = jnp.dot(x, w_up, preferred_element_type=jnp.float32)  24.4 us
    dot_general x1, matrix products, step(): gate = jnp.dot(x, w_gate, preferred_element_type=jnp.float32)  24.3 us
    dot_general x1, matrix products, step(): jnp.dot(hidden, w_down, preferred_element_type=jnp.float32)  23.6 us
    unnamed x5, local copies, waits for them, and re-layouts  8.45 us
  transfers between devices with their start and end apart: 1, of which 1 were waited for; matrix products, arithmetic and copies ran while one was open for 0% of the time, Pallas kernels for 0%

commit v1 on v0

v1 whole, which is shorter than its diff:
```python
import functools

import jax
import jax.numpy as jnp
from jax import lax
from jax.experimental import pallas as pl
from jax.experimental.pallas import tpu as pltpu
from jax.sharding import PartitionSpec as P

MESH = pl.DeviceIdType.MESH
AXIS = "tp"
PIECES = 4
HIDDEN_TILE = 256
WRITES = 8


def kernel(
    n,
    x,
    wg_hbm,
    wu_hbm,
    wd_hbm,
    y,
    wg,
    wu,
    wd,
    xs,
    hidden,
    sums,
    w_sem,
    d_sem,
    x_sem,
    send_sem,
    recv_sem,
):
    rows, depth = x.shape
    width = wg.shape[1]
    columns = wd.shape[1]
    chunk = rows // n
    half = chunk // 2
    tn = columns // PIECES
    th = HIDDEN_TILE
    tiles = width // th
    per_piece = tiles // PIECES

    me = lax.axis_index(AXIS)
    right, left = lax.rem(me + 1, n), lax.rem(me + n - 1, n)
    towards = (right, left)

    def owner(direction, step):
        if direction == 0:
            return lax.rem(me + 2 * n - step, n)
        return lax.rem(me + step, n)

    def row_of(direction, c):
        return pl.multiple_of(c * chunk + direction * half, half)

    def x_copies(step):
        slot = lax.rem(step, 2)
        return [
            pltpu.make_async_copy(
                x.at[pl.ds(row_of(d, owner(d, step)), half), :],
                xs.at[slot, pl.ds(d * half, half), :],
                x_sem.at[slot, d],
            )
            for d in range(2)
        ]

    def w_copies(j):
        cols = pl.ds(pl.multiple_of(j * th, th), th)
        return [
            pltpu.make_async_copy(wg_hbm.at[:, cols], wg.at[:, cols], w_sem.at[0, j]),
            pltpu.make_async_copy(wu_hbm.at[:, cols], wu.at[:, cols], w_sem.at[1, j]),
        ]

    def d_copy(k):
        cols = pl.ds(pl.multiple_of(k * tn, tn), tn)
        return pltpu.make_async_copy(wd_hbm.at[:, cols], wd.at[:, cols], d_sem.at[k])

    def hidden_tile(step, j):
        slot = lax.rem(step, 2)
        cols = pl.ds(pl.multiple_of(j * th, th), th)
        gate = jnp.dot(xs[slot], wg[:, cols], preferred_element_type=jnp.float32)
        up = jnp.dot(xs[slot], wu[:, cols], preferred_element_type=jnp.float32)
        hidden[slot, :, cols] = (jax.nn.gelu(gate) * up).astype(hidden.dtype)

    def term(step, k):
        slot = lax.rem(step, 2)
        cols = pl.ds(pl.multiple_of(k * tn, tn), tn)
        return jnp.dot(hidden[slot], wd[:, cols], preferred_element_type=jnp.float32)

    def reduce_copy(d, step, k):
        return pltpu.make_async_remote_copy(
            src_ref=sums.at[d, step, k],
            dst_ref=sums.at[d, step + 1, k],
            send_sem=send_sem.at[d, step, k],
            recv_sem=recv_sem.at[d, step, k],
            device_id={AXIS: towards[d]},
            device_id_type=MESH,
        )

    def gather_copy(d, hop, k):
        at = y.at[
            pl.ds(row_of(d, owner(d, n - 1 + hop)), half),
            pl.ds(pl.multiple_of(k * tn, tn), tn),
        ]
        return pltpu.make_async_remote_copy(
            src_ref=at,
            dst_ref=at,
            send_sem=send_sem.at[d, n - 1 + hop, k],
            recv_sem=recv_sem.at[d, n - 1 + hop, k],
            device_id={AXIS: towards[d]},
            device_id_type=MESH,
        )

    for copy in x_copies(0):
        copy.start()

    @pl.loop(0, tiles)
    def _(j):
        for copy in w_copies(j):
            copy.start()

    @pl.loop(0, PIECES)
    def _(k):
        d_copy(k).start()

    for copy in x_copies(1):
        copy.start()

    barrier = pltpu.get_barrier_semaphore()
    for neighbour in (left, right):
        pl.semaphore_signal(
            barrier, inc=1, device_id={AXIS: neighbour}, device_id_type=MESH
        )

    for copy in x_copies(0):
        copy.wait()

    @pl.loop(0, tiles)
    def _(j):
        for copy in w_copies(j):
            copy.wait()
        hidden_tile(0, j)

    pl.semaphore_wait(barrier, 2)

    def next_hidden(step, k):
        @pl.loop(0, per_piece)
        def _(i):
            hidden_tile(step + 1, k * per_piece + i)

    for copy in x_copies(1):
        copy.wait()

    @pl.loop(0, PIECES)
    def _(k):
        d_copy(k).wait()
        value = term(0, k).astype(sums.dtype)
        for d in range(2):
            sums[d, 0, k] = value[d * half : (d + 1) * half]
        for d in range(2):
            reduce_copy(d, 0, k).start()
        next_hidden(0, k)

    @pl.loop(1, n - 1)
    def _(step):
        for copy in x_copies(step + 1):
            copy.start()
        for copy in x_copies(step + 1):
            copy.wait()

        @pl.loop(0, PIECES)
        def _(k):
            value = term(step, k)
            for d in range(2):
                reduce_copy(d, step - 1, k).wait_recv()
                part = value[d * half : (d + 1) * half]
                sums[d, step, k] = (
                    sums[d, step, k].astype(jnp.float32) + part
                ).astype(sums.dtype)
                reduce_copy(d, step, k).start()
            next_hidden(step, k)

    @pl.loop(0, PIECES)
    def _(k):
        value = term(n - 1, k)
        for d in range(2):
            reduce_copy(d, n - 2, k).wait_recv()
            part = value[d * half : (d + 1) * half]
            y[
                pl.ds(row_of(d, owner(d, n - 1)), half),
                pl.ds(pl.multiple_of(k * tn, tn), tn),
            ] = (sums[d, n - 1, k].astype(jnp.float32) + part).astype(y.dtype)
            gather_copy(d, 0, k).start()

    @pl.loop(1, n - 1)
    def _(hop):
        @pl.loop(0, PIECES)
        def _(k):
            for d in range(2):
                gather_copy(d, hop - 1, k).wait_recv()
                gather_copy(d, hop, k).start()

    @pl.loop(0, PIECES)
    def _(k):
        for d in range(2):
            gather_copy(d, n - 2, k).wait_recv()

    @pl.loop(0, n - 1)
    def _(step):
        @pl.loop(0, PIECES)
        def _(k):
            for d in range(2):
                reduce_copy(d, step, k).wait_send()
                gather_copy(d, step, k).wait_send()


def write_out(y, out, sem):
    rows = y.shape[0] // WRITES
    copies = [
        pltpu.make_async_copy(
            y.at[pl.ds(i * rows, rows), :], out.at[pl.ds(i * rows, rows), :], sem.at[i]
        )
        for i in range(WRITES)
    ]
    for copy in copies:
        copy.start()
    for copy in copies:
        copy.wait()


def solution(mesh):
    n = mesh.shape[AXIS]

    def step(x, w_gate, w_up, w_down):
        rows, depth = x.shape
        width, columns = w_down.shape
        chunk = rows // n
        half = chunk // 2
        tn = columns // PIECES
        tiles = width // HIDDEN_TILE
        dtype = x.dtype
        hbm = pl.BlockSpec(memory_space=pltpu.HBM)
        gathered = pl.pallas_call(
            functools.partial(kernel, n),
            out_shape=jax.ShapeDtypeStruct((rows, columns), dtype),
            in_specs=[hbm] * 4,
            out_specs=pl.BlockSpec(memory_space=pltpu.VMEM),
            scratch_shapes=[
                pltpu.VMEM(w_gate.shape, dtype),
                pltpu.VMEM(w_up.shape, dtype),
                pltpu.VMEM(w_down.shape, dtype),
                pltpu.VMEM((2, chunk, depth), dtype),
                pltpu.VMEM((2, chunk, width), dtype),
                pltpu.VMEM((2, n, PIECES, half, tn), dtype),
                pltpu.SemaphoreType.DMA((2, tiles)),
                pltpu.SemaphoreType.DMA((PIECES,)),
                pltpu.SemaphoreType.DMA((2, 2)),
                pltpu.SemaphoreType.DMA((2, 2 * n - 2, PIECES)),
                pltpu.SemaphoreType.DMA((2, 2 * n - 2, PIECES)),
            ],
            compiler_params=pltpu.CompilerParams(
                collective_id=0,
                has_side_effects=True,
                vmem_limit_bytes=45 * 1024 * 1024,
            ),
            cost_estimate=pl.CostEstimate(
                flops=6 * rows * depth * width,
                bytes_accessed=2 * (rows * depth * 2 + 3 * depth * width),
                transcendentals=rows * width,
            ),
            name="mlp_ring",
        )(x, w_gate, w_up, w_down)
        return pl.pallas_call(
            write_out,
            out_shape=jax.ShapeDtypeStruct((rows, columns), dtype),
            in_specs=[pl.BlockSpec(memory_space=pltpu.VMEM)],
            out_specs=hbm,
            scratch_shapes=[pltpu.SemaphoreType.DMA((WRITES,))],
            compiler_params=pltpu.CompilerParams(vmem_limit_bytes=12 * 1024 * 1024),
            name="write_out",
        )(gathered)

    return jax.shard_map(
        step,
        mesh=mesh,
        in_specs=(P("dp", None), P(None, AXIS), P(None, AXIS), P(AXIS, None)),
        out_specs=P("dp", None),
        check_vma=False,
    )
```

time: 280 us -> 182 us (0.65)
  waiting for transfers between devices: 186 us -> 0 us
  Pallas kernels: 0 us -> 182 us
  matrix products: 72.2 us -> 0 us
  between operations: 13.4 us -> 0.01 us
  local copies, waits for them, and re-layouts: 8.45 us -> 0 us
    psum x1 -> x0, waiting for transfers between devices: 186 us -> none  [step(): return lax.psum(term, 'tp')]
    pallas_call x0 -> x2, Pallas kernels: none -> 182 us  [the longest x1 178 us: step(): pl.pallas_call(functools.partial(kernel, n), out_shape=jax.ShapeDtypeStru...]
    dot_general x3 -> x0, matrix products: 72.2 us -> none  [the longest x1 24.4 us: step(): up = jnp.dot(x, w_up, preferred_element_type=jnp.float32)]
    unnamed x5 -> x0, local copies, waits for them, and re-layouts: 8.45 us -> none
  transfers between devices with their start and end apart: 1 -> 0, of which waited for: 1 -> 0; matrix products, arithmetic and copies ran while one was open for 0% -> 0% of each run, Pallas kernels for 0% -> 0%
where the time goes in v1:
time: 182 us
  Pallas kernels  182 us (100%)
    pallas_call x1, Pallas kernels, step(): pl.pallas_call(functools.partial(kernel, n), out_shape=jax.ShapeDtypeStru...  178 us

profile of v1, /device:TPU:21, one launch (start us, length us, event | category | flops | bytes accessed | tf_op | source)
XLA Modules:
  0.0 181.5 jit_solution(11111035768176731857)
XLA Ops:
  0.0 178.2 %mlp_ring.1.y = bf16[2048,2048]{1,0:T(8,128)(2,1)S(1)} custom-call(bf16[2048,2048]{1,0:T(8,128)(2,1)} %x.1, bf16[2048,2048]{1,0:T(8,128)(2,1)} %wg_hbm.1, bf16[2048,2048]{1,0:T(8,128)(2,1)} %wu_hbm.1, bf16[2048,2048]{1,0:T(8,128)(2,1)} %wd_hbm.1), custom_call_target="tpu_custom_call" | custom-call | flops 51539607552 | bytes 41943040 | tf_op jit(solution)/shard_map/mlp_ring/pallas_call | solution.py:245
  178.2 3.4 %write_out.1 = bf16[2048,2048]{1,0:T(8,128)(2,1)} custom-call(bf16[2048,2048]{1,0:T(8,128)(2,1)S(1)} %mlp_ring.1.y), custom_call_target="tpu_custom_call" | custom-call | tf_op jit(solution)/shard_map/write_out/pallas_call | solution.py:275

commit v2 on v1

--- a/solution.py
+++ b/solution.py
@@ -10,7 +10,8 @@
 MESH = pl.DeviceIdType.MESH
 AXIS = "tp"
 PIECES = 4
-HIDDEN_TILE = 256
+HIDDEN_TILE = 512
+FIRST_TILES = 4
 WRITES = 8
 
 
@@ -30,8 +31,8 @@
     w_sem,
     d_sem,
     x_sem,
-    send_sem,
     recv_sem,
+    credit_sem,
 ):
     rows, depth = x.shape
     width = wg.shape[1]
@@ -42,6 +43,9 @@
     th = HIDDEN_TILE
     tiles = width // th
     per_piece = tiles // PIECES
+    tw = width // FIRST_TILES
+    last = 2 * n - 3
+    send_sem = w_sem
 
     me = lax.axis_index(AXIS)
     right, left = lax.rem(me + 1, n), lax.rem(me + n - 1, n)
@@ -67,7 +71,7 @@
         ]
 
     def w_copies(j):
-        cols = pl.ds(pl.multiple_of(j * th, th), th)
+        cols = pl.ds(pl.multiple_of(j * tw, tw), tw)
         return [
             pltpu.make_async_copy(wg_hbm.at[:, cols], wg.at[:, cols], w_sem.at[0, j]),
             pltpu.make_async_copy(wu_hbm.at[:, cols], wu.at[:, cols], w_sem.at[1, j]),
@@ -89,34 +93,41 @@
         cols = pl.ds(pl.multiple_of(k * tn, tn), tn)
         return jnp.dot(hidden[slot], wd[:, cols], preferred_element_type=jnp.float32)
 
-    def reduce_copy(d, step, k):
+    def message(d, m, k, src, dst):
         return pltpu.make_async_remote_copy(
-            src_ref=sums.at[d, step, k],
-            dst_ref=sums.at[d, step + 1, k],
-            send_sem=send_sem.at[d, step, k],
-            recv_sem=recv_sem.at[d, step, k],
+            src_ref=src,
+            dst_ref=dst,
+            send_sem=send_sem.at[d, k],
+            recv_sem=recv_sem.at[d, lax.rem(m, 2), k],
             device_id={AXIS: towards[d]},
             device_id_type=MESH,
         )
+
+    def reduce_copy(d, step, k):
+        return message(d, step, k, sums.at[d, step, k], sums.at[d, step + 1, k])
 
     def gather_copy(d, hop, k):
         at = y.at[
             pl.ds(row_of(d, owner(d, n - 1 + hop)), half),
             pl.ds(pl.multiple_of(k * tn, tn), tn),
         ]
-        return pltpu.make_async_remote_copy(
-            src_ref=at,
-            dst_ref=at,
-            send_sem=send_sem.at[d, n - 1 + hop, k],
-            recv_sem=recv_sem.at[d, n - 1 + hop, k],
-            device_id={AXIS: towards[d]},
+        return message(d, n - 1 + hop, k, at, at)
+
+    def give_credit(d, k):
+        pl.semaphore_signal(
+            credit_sem.at[d, k],
+            inc=1,
+            device_id={AXIS: towards[1 - d]},
             device_id_type=MESH,
         )
 
+    def take_credit(d, k):
+        pl.semaphore_wait(credit_sem.at[d, k], 1)
+
     for copy in x_copies(0):
         copy.start()
 
-    @pl.loop(0, tiles)
+    @pl.loop(0, FIRST_TILES)
     def _(j):
         for copy in w_copies(j):
             copy.start()
@@ -125,8 +136,10 @@
     def _(k):
         d_copy(k).start()
 
-    for copy in x_copies(1):
-        copy.start()
+        @pl.when(k == 0)
+        def _():
+            for copy in x_copies(1):
+                copy.start()
 
     barrier = pltpu.get_barrier_semaphore()
     for neighbour in (left, right):
@@ -137,7 +150,7 @@
     for copy in x_copies(0):
         copy.wait()
 
-    @pl.loop(0, tiles)
+    @pl.loop(0, FIRST_TILES)
     def _(j):
         for copy in w_copies(j):
             copy.wait()
@@ -149,9 +162,6 @@
         @pl.loop(0, per_piece)
         def _(i):
             hidden_tile(step + 1, k * per_piece + i)
-
-    for copy in x_copies(1):
-        copy.wait()
 
     @pl.loop(0, PIECES)
     def _(k):
@@ -161,12 +171,19 @@
             sums[d, 0, k] = value[d * half : (d + 1) * half]
         for d in range(2):
             reduce_copy(d, 0, k).start()
+
+        @pl.when(k == 0)
+        def _():
+            for copy in x_copies(1):
+                copy.wait()
+
         next_hidden(0, k)
+
+    for copy in x_copies(2):
+        copy.start()
 
     @pl.loop(1, n - 1)
     def _(step):
-        for copy in x_copies(step + 1):
-            copy.start()
         for copy in x_copies(step + 1):
             copy.wait()
 
@@ -174,24 +191,37 @@
         def _(k):
             value = term(step, k)
             for d in range(2):
-                reduce_copy(d, step - 1, k).wait_recv()
+                reduce_copy(d, step - 1, k).wait()
+                give_credit(d, k)
                 part = value[d * half : (d + 1) * half]
                 sums[d, step, k] = (
                     sums[d, step, k].astype(jnp.float32) + part
                 ).astype(sums.dtype)
+
+                @pl.when(step >= 2)
+                def _():
+                    take_credit(d, k)
+
                 reduce_copy(d, step, k).start()
             next_hidden(step, k)
+
+        @pl.when(step < n - 2)
+        def _():
+            for copy in x_copies(step + 2):
+                copy.start()
 
     @pl.loop(0, PIECES)
     def _(k):
         value = term(n - 1, k)
         for d in range(2):
-            reduce_copy(d, n - 2, k).wait_recv()
+            reduce_copy(d, n - 2, k).wait()
+            give_credit(d, k)
             part = value[d * half : (d + 1) * half]
             y[
                 pl.ds(row_of(d, owner(d, n - 1)), half),
                 pl.ds(pl.multiple_of(k * tn, tn), tn),
             ] = (sums[d, n - 1, k].astype(jnp.float32) + part).astype(y.dtype)
+            take_credit(d, k)
             gather_copy(d, 0, k).start()
 
     @pl.loop(1, n - 1)
@@ -199,21 +229,18 @@
         @pl.loop(0, PIECES)
         def _(k):
             for d in range(2):
-                gather_copy(d, hop - 1, k).wait_recv()
+                gather_copy(d, hop - 1, k).wait()
+                take_credit(d, k)
                 gather_copy(d, hop, k).start()
+
+                @pl.when(n - 1 + hop - 1 <= last - 2)
+                def _():
+                    give_credit(d, k)
 
     @pl.loop(0, PIECES)
     def _(k):
         for d in range(2):
-            gather_copy(d, n - 2, k).wait_recv()
-
-    @pl.loop(0, n - 1)
-    def _(step):
-        @pl.loop(0, PIECES)
-        def _(k):
-            for d in range(2):
-                reduce_copy(d, step, k).wait_send()
-                gather_copy(d, step, k).wait_send()
+            gather_copy(d, n - 2, k).wait()
 
 
 def write_out(y, out, sem):
@@ -239,7 +266,6 @@
         chunk = rows // n
         half = chunk // 2
         tn = columns // PIECES
-        tiles = width // HIDDEN_TILE
         dtype = x.dtype
         hbm = pl.BlockSpec(memory_space=pltpu.HBM)
         gathered = pl.pallas_call(
@@ -254,11 +280,11 @@
                 pltpu.VMEM((2, chunk, depth), dtype),
                 pltpu.VMEM((2, chunk, width), dtype),
                 pltpu.VMEM((2, n, PIECES, half, tn), dtype),
-                pltpu.SemaphoreType.DMA((2, tiles)),
+                pltpu.SemaphoreType.DMA((2, FIRST_TILES)),
                 pltpu.SemaphoreType.DMA((PIECES,)),
                 pltpu.SemaphoreType.DMA((2, 2)),
-                pltpu.SemaphoreType.DMA((2, 2 * n - 2, PIECES)),
-                pltpu.SemaphoreType.DMA((2, 2 * n - 2, PIECES)),
+                pltpu.SemaphoreType.DMA((2, 2, PIECES)),
+                pltpu.SemaphoreType.REGULAR((2, PIECES)),
             ],
             compiler_params=pltpu.CompilerParams(
                 collective_id=0,

time: 182 us -> 178 us (0.978)
  Pallas kernels: 182 us -> 178 us
    pallas_call x1, Pallas kernels: 178 us -> 174 us  [step(): pl.pallas_call(functools.partial(kernel, n), out_shape=jax.ShapeDtypeStru...]
where the time goes in v2:
time: 178 us
  Pallas kernels  178 us (100%)
    pallas_call x1, Pallas kernels, step(): pl.pallas_call(functools.partial(kernel, n), out_shape=jax.ShapeDtypeStru...  174 us

profile of v2, /device:TPU:21, one launch (start us, length us, event | category | flops | bytes accessed | tf_op | source)
XLA Modules:
  0.0 177.7 jit_solution(8558440336240675941)
XLA Ops:
  0.0 174.3 %mlp_ring.1.y = bf16[2048,2048]{1,0:T(8,128)(2,1)S(1)} custom-call(bf16[2048,2048]{1,0:T(8,128)(2,1)} %x.1, bf16[2048,2048]{1,0:T(8,128)(2,1)} %wg_hbm.1, bf16[2048,2048]{1,0:T(8,128)(2,1)} %wu_hbm.1, bf16[2048,2048]{1,0:T(8,128)(2,1)} %wd_hbm.1), custom_call_target="tpu_custom_call" | custom-call | flops 51539607552 | bytes 41943040 | tf_op jit(solution)/shard_map/mlp_ring/pallas_call | solution.py:271
  174.3 3.4 %write_out.1 = bf16[2048,2048]{1,0:T(8,128)(2,1)} custom-call(bf16[2048,2048]{1,0:T(8,128)(2,1)S(1)} %mlp_ring.1.y), custom_call_target="tpu_custom_call" | custom-call | tf_op jit(solution)/shard_map/write_out/pallas_call | solution.py:301

commit v3 on v2

v3 whole, which is shorter than its diff:
```python
import functools

import jax
import jax.numpy as jnp
from jax import lax
from jax.experimental import pallas as pl
from jax.experimental.pallas import tpu as pltpu
from jax.sharding import PartitionSpec as P

MESH = pl.DeviceIdType.MESH
AXIS = "tp"
PARTS = 2
PIECES = 2
SHARES = 2
FIRST_TILES = 4
WRITES = 4


def kernel(
    n,
    x,
    wg_hbm,
    wu_hbm,
    wd_hbm,
    y,
    wg,
    wu,
    wd,
    xs,
    hidden,
    sums,
    w_sem,
    d_sem,
    x_sem,
    recv_sem,
    credit_sem,
):
    rows, depth = x.shape
    width = wg.shape[1]
    columns = wd.shape[1]
    chunk = rows // n
    half = chunk // 2
    part = half // PARTS
    units = n * PARTS
    tn = columns // PIECES
    tw = width // FIRST_TILES
    th = width // PIECES
    tf = tn // SHARES
    firsts = PIECES * SHARES
    last = 2 * n - 3
    send_sem = w_sem

    me = lax.axis_index(AXIS)
    right, left = lax.rem(me + 1, n), lax.rem(me + n - 1, n)
    towards = (right, left)

    def owner(direction, step):
        if direction == 0:
            return lax.rem(me + 2 * n - step, n)
        return lax.rem(me + step, n)

    def row_of(direction, step, p):
        row = owner(direction, step) * chunk + direction * half + p * part
        return pl.multiple_of(row, part)

    def columns_of(k, size=tn):
        return pl.ds(pl.multiple_of(k * size, size), size)

    def x_copies(unit):
        slot = lax.rem(unit, 2)
        step, p = lax.div(unit, PARTS), lax.rem(unit, PARTS)
        return [
            pltpu.make_async_copy(
                x.at[pl.ds(row_of(d, step, p), part), :],
                xs.at[slot, pl.ds(d * part, part), :],
                x_sem.at[slot, d],
            )
            for d in range(2)
        ]

    def w_copies(j):
        cols = pl.ds(pl.multiple_of(j * tw, tw), tw)
        return [
            pltpu.make_async_copy(wg_hbm.at[:, cols], wg.at[:, cols], w_sem.at[0, j]),
            pltpu.make_async_copy(wu_hbm.at[:, cols], wu.at[:, cols], w_sem.at[1, j]),
        ]

    def d_copy(k):
        cols = columns_of(k, tf)
        return pltpu.make_async_copy(wd_hbm.at[:, cols], wd.at[:, cols], d_sem.at[k])

    def hidden_tile(unit, j, size):
        slot = lax.rem(unit, 2)
        cols = pl.ds(pl.multiple_of(j * size, size), size)
        gate = jnp.dot(xs[slot], wg[:, cols], preferred_element_type=jnp.float32)
        up = jnp.dot(xs[slot], wu[:, cols], preferred_element_type=jnp.float32)
        hidden[slot, :, cols] = (jax.nn.gelu(gate) * up).astype(hidden.dtype)

    def term(unit, cols):
        slot = lax.rem(unit, 2)
        return jnp.dot(hidden[slot], wd[:, cols], preferred_element_type=jnp.float32)

    def message(d, m, p, k, src, dst):
        piece = p * PIECES + k
        return pltpu.make_async_remote_copy(
            src_ref=src,
            dst_ref=dst,
            send_sem=send_sem.at[d, piece],
            recv_sem=recv_sem.at[d, lax.rem(m, 2), piece],
            device_id={AXIS: towards[d]},
            device_id_type=MESH,
        )

    def reduce_copy(d, step, p, k):
        return message(
            d, step, p, k, sums.at[d, step, p, k], sums.at[d, step + 1, p, k]
        )

    def first_copy(d, p, k, share):
        cols = columns_of(share, tf)
        return message(
            d, 0, p, k, sums.at[d, 0, p, k, :, cols], sums.at[d, 1, p, k, :, cols]
        )

    def gather_copy(d, hop, p, k):
        at = y.at[pl.ds(row_of(d, n - 1 + hop, p), part), columns_of(k)]
        return message(d, n - 1 + hop, p, k, at, at)

    def give_credit(d):
        pl.semaphore_signal(
            credit_sem.at[d],
            inc=1,
            device_id={AXIS: towards[1 - d]},
            device_id_type=MESH,
        )

    def take_credit(d):
        pl.semaphore_wait(credit_sem.at[d], 1)

    for copy in x_copies(0):
        copy.start()

    @pl.loop(0, FIRST_TILES)
    def _(j):
        for copy in w_copies(j):
            copy.start()

    @pl.loop(0, firsts)
    def _(k):
        d_copy(k).start()

        @pl.when(k == 0)
        def _():
            for copy in x_copies(1):
                copy.start()

    barrier = pltpu.get_barrier_semaphore()
    for neighbour in (left, right):
        pl.semaphore_signal(
            barrier, inc=1, device_id={AXIS: neighbour}, device_id_type=MESH
        )

    for copy in x_copies(0):
        copy.wait()

    @pl.loop(0, FIRST_TILES)
    def _(j):
        for copy in w_copies(j):
            copy.wait()
        hidden_tile(0, j, tw)

    pl.semaphore_wait(barrier, 2)

    def next_hidden(unit, k, size=th):
        @pl.when(k == 0)
        def _():
            for copy in x_copies(unit + 1):
                copy.wait()

        hidden_tile(unit + 1, k, size)

    def fetch(unit):
        for copy in x_copies(unit):
            copy.start()

    @pl.loop(0, PARTS)
    def _(unit):
        @pl.loop(0, firsts)
        def _(f):
            k, share = lax.div(f, SHARES), lax.rem(f, SHARES)

            @pl.when(unit == 0)
            def _():
                d_copy(f).wait()

            value = term(unit, columns_of(f, tf)).astype(sums.dtype)
            for d in range(2):
                sums[d, 0, unit, k, :, columns_of(share, tf)] = value[
                    d * part : (d + 1) * part
                ]
            for d in range(2):
                first_copy(d, unit, k, share).start()
            next_hidden(unit, f, width // firsts)

            @pl.when(f == 0)
            def _():
                fetch(unit + 2)

    @pl.loop(PARTS, units - PARTS)
    def _(unit):
        step, p = lax.div(unit, PARTS), lax.rem(unit, PARTS)

        fetch(unit + 2)

        @pl.loop(0, PIECES)
        def _(k):
            value = term(unit, columns_of(k))
            for d in range(2):
                reduce_copy(d, step - 1, p, k).wait()
                give_credit(d)
                sums[d, step, p, k] = (
                    sums[d, step, p, k].astype(jnp.float32)
                    + value[d * part : (d + 1) * part]
                ).astype(sums.dtype)

                @pl.when(step >= 2)
                def _():
                    take_credit(d)

                reduce_copy(d, step, p, k).start()
            next_hidden(unit, k)

    @pl.loop(units - PARTS, units)
    def _(unit):
        p = lax.rem(unit, PARTS)

        @pl.loop(0, PIECES)
        def _(k):
            value = term(unit, columns_of(k))
            for d in range(2):
                reduce_copy(d, n - 2, p, k).wait()
                give_credit(d)
                y[pl.ds(row_of(d, n - 1, p), part), columns_of(k)] = (
                    sums[d, n - 1, p, k].astype(jnp.float32)
                    + value[d * part : (d + 1) * part]
                ).astype(y.dtype)
                take_credit(d)
                gather_copy(d, 0, p, k).start()

            @pl.when(unit < units - 1)
            def _():
                next_hidden(unit, k)

    @pl.loop(1, n - 1)
    def _(hop):
        @pl.loop(0, PARTS)
        def _(p):
            @pl.loop(0, PIECES)
            def _(k):
                for d in range(2):
                    gather_copy(d, hop - 1, p, k).wait()
                    take_credit(d)
                    gather_copy(d, hop, p, k).start()

                    @pl.when(n - 1 + hop - 1 <= last - 2)
                    def _():
                        give_credit(d)

    @pl.loop(0, PARTS)
    def _(p):
        @pl.loop(0, PIECES)
        def _(k):
            for d in range(2):
                gather_copy(d, n - 2, p, k).wait()


def write_out(y, out, sem):
    rows = y.shape[0] // WRITES
    copies = [
        pltpu.make_async_copy(
            y.at[pl.ds(i * rows, rows), :], out.at[pl.ds(i * rows, rows), :], sem.at[i]
        )
        for i in range(WRITES)
    ]
    for copy in copies:
        copy.start()
    for copy in copies:
        copy.wait()


def solution(mesh):
    n = mesh.shape[AXIS]

    def step(x, w_gate, w_up, w_down):
        rows, depth = x.shape
        width, columns = w_down.shape
        half = rows // n // 2
        part = half // PARTS
        tn = columns // PIECES
        dtype = x.dtype
        hbm = pl.BlockSpec(memory_space=pltpu.HBM)
        gathered = pl.pallas_call(
            functools.partial(kernel, n),
            out_shape=jax.ShapeDtypeStruct((rows, columns), dtype),
            in_specs=[hbm] * 4,
            out_specs=pl.BlockSpec(memory_space=pltpu.VMEM),
            scratch_shapes=[
                pltpu.VMEM(w_gate.shape, dtype),
                pltpu.VMEM(w_up.shape, dtype),
                pltpu.VMEM(w_down.shape, dtype),
                pltpu.VMEM((2, 2 * part, depth), dtype),
                pltpu.VMEM((2, 2 * part, width), dtype),
                pltpu.VMEM((2, n, PARTS, PIECES, part, tn), dtype),
                pltpu.SemaphoreType.DMA((2, FIRST_TILES)),
                pltpu.SemaphoreType.DMA((PIECES * SHARES,)),
                pltpu.SemaphoreType.DMA((2, 2)),
                pltpu.SemaphoreType.DMA((2, 2, PARTS * PIECES)),
                pltpu.SemaphoreType.REGULAR((2,)),
            ],
            compiler_params=pltpu.CompilerParams(
                collective_id=0,
                has_side_effects=True,
                vmem_limit_bytes=45 * 1024 * 1024,
            ),
            cost_estimate=pl.CostEstimate(
                flops=6 * rows * depth * width,
                bytes_accessed=2 * (rows * depth * 2 + 3 * depth * width),
                transcendentals=rows * width,
            ),
            name="mlp_ring",
        )(x, w_gate, w_up, w_down)
        return pl.pallas_call(
            write_out,
            out_shape=jax.ShapeDtypeStruct((rows, columns), dtype),
            in_specs=[pl.BlockSpec(memory_space=pltpu.VMEM)],
            out_specs=hbm,
            scratch_shapes=[pltpu.SemaphoreType.DMA((WRITES,))],
            compiler_params=pltpu.CompilerParams(vmem_limit_bytes=12 * 1024 * 1024),
            name="write_out",
        )(gathered)

    return jax.shard_map(
        step,
        mesh=mesh,
        in_specs=(P("dp", None), P(None, AXIS), P(None, AXIS), P(AXIS, None)),
        out_specs=P("dp", None),
        check_vma=False,
    )
```

time: 178 us -> 177 us (level)
  no operation moved by 1% of the time
where the time goes in v3:
time: 177 us
  Pallas kernels  177 us (100%)
    pallas_call x1, Pallas kernels, step(): pl.pallas_call(functools.partial(kernel, n), out_shape=jax.ShapeDtypeStru...  174 us

profile of v3, /device:TPU:21, one launch (start us, length us, event | category | flops | bytes accessed | tf_op | source)
XLA Modules:
  0.0 177.0 jit_solution(12985056891482914408)
XLA Ops:
  0.0 173.7 %mlp_ring.1.y = bf16[2048,2048]{1,0:T(8,128)(2,1)S(1)} custom-call(bf16[2048,2048]{1,0:T(8,128)(2,1)} %x.1, bf16[2048,2048]{1,0:T(8,128)(2,1)} %wg_hbm.1, bf16[2048,2048]{1,0:T(8,128)(2,1)} %wu_hbm.1, bf16[2048,2048]{1,0:T(8,128)(2,1)} %wd_hbm.1), custom_call_target="tpu_custom_call" | custom-call | flops 51539607552 | bytes 41943040 | tf_op jit(solution)/shard_map/mlp_ring/pallas_call | solution.py:302
  173.7 3.4 %write_out.1 = bf16[2048,2048]{1,0:T(8,128)(2,1)} custom-call(bf16[2048,2048]{1,0:T(8,128)(2,1)S(1)} %mlp_ring.1.y), custom_call_target="tpu_custom_call" | custom-call | tf_op jit(solution)/shard_map/write_out/pallas_call | solution.py:332

commit v4 on v3

--- a/solution.py
+++ b/solution.py
@@ -10,9 +10,9 @@
 MESH = pl.DeviceIdType.MESH
 AXIS = "tp"
 PARTS = 2
-PIECES = 2
-SHARES = 2
-FIRST_TILES = 4
+PIECES = 1
+SHARES = 4
+FIRST_TILES = 8
 WRITES = 4
 
 
@@ -44,7 +44,7 @@
     units = n * PARTS
     tn = columns // PIECES
     tw = width // FIRST_TILES
-    th = width // PIECES
+    th = width // 2
     tf = tn // SHARES
     firsts = PIECES * SHARES
     last = 2 * n - 3
@@ -85,9 +85,10 @@
             pltpu.make_async_copy(wu_hbm.at[:, cols], wu.at[:, cols], w_sem.at[1, j]),
         ]
 
-    def d_copy(k):
-        cols = columns_of(k, tf)
-        return pltpu.make_async_copy(wd_hbm.at[:, cols], wd.at[:, cols], d_sem.at[k])
+    def d_copy(k, size=tf):
+        cols = columns_of(k, size)
+        sem = d_sem.at[k] if size == tf else d_sem.at[k * firsts]
+        return pltpu.make_async_copy(wd_hbm.at[:, cols], wd.at[:, cols], sem)
 
     def hidden_tile(unit, j, size):
         slot = lax.rem(unit, 2)
@@ -116,8 +117,8 @@
             d, step, p, k, sums.at[d, step, p, k], sums.at[d, step + 1, p, k]
         )
 
-    def first_copy(d, p, k, share):
-        cols = columns_of(share, tf)
+    def first_copy(d, p, k, share, size=tf):
+        cols = columns_of(share, size)
         return message(
             d, 0, p, k, sums.at[d, 0, p, k, :, cols], sums.at[d, 1, p, k, :, cols]
         )
@@ -145,14 +146,16 @@
         for copy in w_copies(j):
             copy.start()
 
-    @pl.loop(0, firsts)
+    @pl.loop(0, 2)
+    def _(k):
+        d_copy(k, tf // 2).start()
+
+    for copy in x_copies(1):
+        copy.start()
+
+    @pl.loop(1, firsts)
     def _(k):
         d_copy(k).start()
-
-        @pl.when(k == 0)
-        def _():
-            for copy in x_copies(1):
-                copy.start()
 
     barrier = pltpu.get_barrier_semaphore()
     for neighbour in (left, right):
@@ -183,9 +186,22 @@
         for copy in x_copies(unit):
             copy.start()
 
+    @pl.loop(0, 2)
+    def _(f):
+        d_copy(f, tf // 2).wait()
+        value = term(0, columns_of(f, tf // 2)).astype(sums.dtype)
+        for d in range(2):
+            sums[d, 0, 0, 0, :, columns_of(f, tf // 2)] = value[
+                d * part : (d + 1) * part
+            ]
+        for d in range(2):
+            first_copy(d, 0, 0, f, tf // 2).start()
+
+    fetch(2)
+
     @pl.loop(0, PARTS)
     def _(unit):
-        @pl.loop(0, firsts)
+        @pl.loop(jnp.where(unit == 0, 1, 0), firsts)
         def _(f):
             k, share = lax.div(f, SHARES), lax.rem(f, SHARES)
 
@@ -200,11 +216,15 @@
                 ]
             for d in range(2):
                 first_copy(d, unit, k, share).start()
-            next_hidden(unit, f, width // firsts)
+            next_hidden(unit, jnp.where(unit == 0, f - 1, f), width // firsts)
 
             @pl.when(f == 0)
             def _():
                 fetch(unit + 2)
+
+        @pl.when(unit == 0)
+        def _():
+            next_hidden(unit, jnp.int32(firsts - 1), width // firsts)
 
     @pl.loop(PARTS, units - PARTS)
     def _(unit):
@@ -228,7 +248,8 @@
                     take_credit(d)
 
                 reduce_copy(d, step, p, k).start()
-            next_hidden(unit, k)
+            for tile in range(2):
+                next_hidden(unit, jnp.int32(tile))
 
     @pl.loop(units - PARTS, units)
     def _(unit):
@@ -249,7 +270,8 @@
 
             @pl.when(unit < units - 1)
             def _():
-                next_hidden(unit, k)
+                for tile in range(2):
+                    next_hidden(unit, jnp.int32(tile))
 
     @pl.loop(1, n - 1)
     def _(hop):
@@ -312,7 +334,7 @@
                 pltpu.VMEM((2, 2 * part, width), dtype),
                 pltpu.VMEM((2, n, PARTS, PIECES, part, tn), dtype),
                 pltpu.SemaphoreType.DMA((2, FIRST_TILES)),
-                pltpu.SemaphoreType.DMA((PIECES * SHARES,)),
+                pltpu.SemaphoreType.DMA((PIECES * SHARES + 1,)),
                 pltpu.SemaphoreType.DMA((2, 2)),
                 pltpu.SemaphoreType.DMA((2, 2, PARTS * PIECES)),
                 pltpu.SemaphoreType.REGULAR((2,)),

time: 177 us -> 176 us (level)
  no operation moved by 1% of the time
where the time goes in v4:
time: 176 us
  Pallas kernels  176 us (100%)
    pallas_call x1, Pallas kernels, step(): pl.pallas_call(functools.partial(kernel, n), out_shape=jax.ShapeDtypeStru...  173 us

profile of v4, /device:TPU:21, one launch (start us, length us, event | category | flops | bytes accessed | tf_op | source)
XLA Modules:
  0.0 176.4 jit_solution(5825552405846194277)
XLA Ops:
  0.0 173.0 %mlp_ring.1.y = bf16[2048,2048]{1,0:T(8,128)(2,1)S(1)} custom-call(bf16[2048,2048]{1,0:T(8,128)(2,1)} %x.1, bf16[2048,2048]{1,0:T(8,128)(2,1)} %wg_hbm.1, bf16[2048,2048]{1,0:T(8,128)(2,1)} %wu_hbm.1, bf16[2048,2048]{1,0:T(8,128)(2,1)} %wd_hbm.1), custom_call_target="tpu_custom_call" | custom-call | flops 51539607552 | bytes 41943040 | tf_op jit(solution)/shard_map/mlp_ring/pallas_call | solution.py:324
  173.1 3.4 %write_out.1 = bf16[2048,2048]{1,0:T(8,128)(2,1)} custom-call(bf16[2048,2048]{1,0:T(8,128)(2,1)S(1)} %mlp_ring.1.y), custom_call_target="tpu_custom_call" | custom-call | tf_op jit(solution)/shard_map/write_out/pallas_call | solution.py:354
